TPU v7x, 32 devices: a 4x4x1 block of a 4x4x8 slice. The times are simulated.
32 devices in a mesh: dp: 1 (over z), tp: 32 (over x, y, core).
Axes of the slice: x: 4, y: 4, z: 1, core: 2. Of those that a mesh axis runs over, the one named last changes fastest.
The devices are a block of a 4x4x8 slice.
Arguments:
- x: bfloat16 [2048, 4096], P('dp')
- dy: bfloat16 [2048, 4096], P('dp')
- gate: bfloat16 [2048, 12288], P('dp', 'tp')
- up: bfloat16 [2048, 12288], P('dp', 'tp')
- w_gate: bfloat16 [4096, 12288], P(None, 'tp')
- w_up: bfloat16 [4096, 12288], P(None, 'tp')
- w_down: bfloat16 [12288, 4096], P('tp')
Outputs:
- output 1: bfloat16 [2048, 4096], P('dp')
- output 2: bfloat16 [4096, 12288], P('dp', 'tp')
- output 3: bfloat16 [4096, 12288], P('dp', 'tp')
- output 4: bfloat16 [12288, 4096], P(('dp', 'tp'))
All inputs are finite; a program needn't handle non-finite values.
Results may differ from a plain program's by a relative error of at most 0.012.
Values are sent between devices in bfloat16 or wider.
A program may use at most 768 MiB of HBM per device.

v0:
```python
import jax
import jax.numpy as jnp
from jax import lax
from jax.sharding import PartitionSpec as P


def act(gate, up):
    return jax.nn.silu(gate) * up


def solution(mesh):
    def step(x, dy, gate, up, w_gate, w_up, w_down):
        hidden, back = jax.vjp(act, gate.astype(jnp.float32), up.astype(jnp.float32))
        d_hidden = jnp.dot(dy, w_down.T, preferred_element_type=jnp.float32)
        d_gate, d_up = (g.astype(jnp.bfloat16) for g in back(d_hidden))
        term = jnp.dot(d_gate, w_gate.T, preferred_element_type=jnp.float32) + jnp.dot(d_up, w_up.T, preferred_element_type=jnp.float32)
        dx = lax.psum(term.astype(jnp.bfloat16), "tp")
        dw_gate = jnp.dot(x.T, d_gate, preferred_element_type=jnp.float32)
        dw_up = jnp.dot(x.T, d_up, preferred_element_type=jnp.float32)
        dw_down = jnp.dot(hidden.astype(jnp.bfloat16).T, dy, preferred_element_type=jnp.float32)
        return dx, *(g.astype(jnp.bfloat16) for g in (dw_gate, dw_up, dw_down))

    tokens, columns, rows = P("dp", None), P(None, "tp"), P("tp", None)
    return jax.shard_map(
        step,
        mesh=mesh,
        in_specs=(tokens, tokens, P("dp", "tp"), P("dp", "tp"), columns, columns, rows),
        out_specs=(tokens, P("dp", "tp"), P("dp", "tp"), P(("dp", "tp"), None)),
        check_vma=False,
    )
```

profile of v0, /device:TPU:97, one launch (start us, length us, event | category | flops | bytes accessed | tf_op | source)
XLA Modules:
  0.0 252.6 jit_solution(3397336588049966060)
XLA Ops:
  7.2 0.0 copy-start
  7.2 0.1 all-reduce.2.cloned.1.call-start
  7.3 16.0 %fusion.8 = (bf16[2048,384]{1,0:T(8,128)(2,1)S(1)}, f32[2048,384]{1,0:T(8,128)}) fusion(bf16[2048,384]{1,0:T(8,128)(2,1)} %param.9, bf16[2048,384]{1,0:T(8,128)(2,1)} %param.10, bf16[2048,4096]{1,0:T(8,128)(2,1)} %param.8, bf16[384,4096]{1,0:T(8,128)(2,1)} %param.13), kind=kOutput, calls=%fused_computation.18 | convolution fusion | flops 6452674560 | bytes 27787264 | tf_op jit(solution)/shard_map/dot_general | solution.py:14
  23.2 0.0 copy-start.3
  23.2 0.0 copy-done
  23.2 14.5 %fusion.11 = f32[2048,4096]{1,0:T(8,128)} fusion(bf16[2048,384]{1,0:T(8,128)(2,1)S(1)} %get-tuple-element.8, bf16[4096,384]{1,0:T(8,128)(2,1)S(1)} %copy-done), kind=kOutput, calls=%fused_computation.21 | convolution fusion | flops 6442450944 | bytes 38273024 | tf_op jit(solution)/shard_map/dot_general | solution.py:16
  37.8 0.0 copy-done.3
  37.8 23.1 %add_convert_fusion = bf16[2048,4096]{1,0:T(8,128)(2,1)} fusion(f32[2048,4096]{1,0:T(8,128)} %fusion.11, bf16[4096,384]{1,0:T(8,128)(2,1)} %param.12, f32[2048,384]{1,0:T(8,128)} %get-tuple-element.9, bf16[2048,384]{1,0:T(8,128)(2,1)} %param.9), kind=kOutput, calls=%fused_computation | convolution fusion | flops 6464733184 | bytes 58195968 | tf_op jit(solution)/shard_map/dot_general | solution.py:16
  60.9 0.0 copy-start.4
  60.9 0.1 all-reduce.2.cloned.1.call-update
  60.9 1.3 copy-done.4
  62.3 11.5 %fusion = bf16[4096,384]{0,1:T(8,128)(2,1)} fusion(bf16[2048,384]{1,0:T(8,128)(2,1)S(1)} %copy-done.4, bf16[2048,4096]{1,0:T(8,128)(2,1)} %param.7), kind=kOutput, calls=%fused_computation.4 | convolution fusion | flops 6444023808 | bytes 21495808 | tf_op jit(solution)/shard_map/dot_general | solution.py:18
  73.8 0.0 copy-start.2
  73.8 4.8 %copy.11 = bf16[4096,384]{1,0:T(8,128)(2,1)} copy(bf16[4096,384]{0,1:T(8,128)(2,1)} %fusion) | data formatting | bytes 6291456
  78.6 0.0 copy-done.2
  78.6 12.6 %fusion.1 = bf16[4096,384]{0,1:T(8,128)(2,1)} fusion(bf16[2048,4096]{1,0:T(8,128)(2,1)} %param.7, f32[2048,384]{1,0:T(8,128)S(1)} %copy-done.2, bf16[2048,384]{1,0:T(8,128)(2,1)} %param.9), kind=kOutput, calls=%fused_computation.5 | convolution fusion | flops 6449528832 | bytes 24641536 | tf_op jit(solution)/shard_map/dot_general | solution.py:19
  91.1 0.0 copy-start.5
  91.1 0.0 copy-start.6
  91.1 4.8 %copy.12 = bf16[4096,384]{1,0:T(8,128)(2,1)} copy(bf16[4096,384]{0,1:T(8,128)(2,1)} %fusion.1) | data formatting | bytes 6291456
  95.9 0.0 copy-done.5
  95.9 0.0 copy-done.6
  95.9 12.2 %convolution_convert_fusion = bf16[384,4096]{1,0:T(8,128)(2,1)} fusion(bf16[2048,4096]{1,0:T(8,128)(2,1)} %param.8, bf16[2048,384]{1,0:T(8,128)(2,1)S(1)} %copy-done.6, bf16[2048,384]{1,0:T(8,128)(2,1)S(1)} %copy-done.5), kind=kOutput, calls=%fused_computation.1 | convolution fusion | flops 6450315264 | bytes 23068672 | tf_op jit(solution)/shard_map/dot_general | solution.py:20
  108.1 123.3 %all-reduce.2.cloned.1.call-done = bf16[2048,4096]{1,0:T(8,128)(2,1)} async-done(((bf16[2048,4096]{1,0:T(8,128)(2,1)}), bf16[2048,4096]{1,0:T(8,128)(2,1)}) %all-reduce.2.cloned.1.call-update) | async-done | bytes 16777232 | tf_op jit(solution)/shard_map/psum | solution.py:17
  231.4 0.0 copy-start.1
  231.4 14.3 %copy.14 = bf16[2048,4096]{1,0:T(8,128)(2,1)} copy(bf16[2048,4096]{1,0:T(8,128)(2,1)} %all-reduce.2.cloned.1.call-done) | data formatting | bytes 33554432
  245.7 0.0 copy-done.1
Async XLA Ops:
  7.2 16.1 %copy-start = (bf16[4096,384]{1,0:T(8,128)(2,1)S(1)}, bf16[4096,384]{1,0:T(8,128)(2,1)}, u32[]{:S(2)}) copy-start(bf16[4096,384]{1,0:T(8,128)(2,1)} %param.11) | copy-start | bytes 9437188
  7.2 224.2 %all-reduce.2.cloned.1.call-start = ((), (), s32[]{:S(2)}) async-start(), calls=%async_computation | async-start | bytes 33554432 | tf_op jit(solution)/shard_map/psum | solution.py:17
  23.2 14.5 %copy-start.3 = (bf16[2048,384]{1,0:T(8,128)(2,1)}, bf16[2048,384]{1,0:T(8,128)(2,1)S(1)}, u32[]{:S(2)}) copy-start(bf16[2048,384]{1,0:T(8,128)(2,1)S(1)} %get-tuple-element.8) | copy-start | bytes 4718596
  60.9 1.4 copy-start.4
  73.8 4.8 %copy-start.2 = (f32[2048,384]{1,0:T(8,128)S(1)}, f32[2048,384]{1,0:T(8,128)}, u32[]{:S(2)}) copy-start(f32[2048,384]{1,0:T(8,128)} %get-tuple-element.9) | copy-start | bytes 9437188
  91.1 4.8 %copy-start.5 = (bf16[2048,384]{1,0:T(8,128)(2,1)S(1)}, bf16[2048,384]{1,0:T(8,128)(2,1)}, u32[]{:S(2)}) copy-start(bf16[2048,384]{1,0:T(8,128)(2,1)} %param.9) | copy-start | bytes 4718596
  91.1 4.8 %copy-start.6 = (bf16[2048,384]{1,0:T(8,128)(2,1)S(1)}, bf16[2048,384]{1,0:T(8,128)(2,1)}, u32[]{:S(2)}) copy-start(bf16[2048,384]{1,0:T(8,128)(2,1)} %param.10) | copy-start | bytes 4718596
  231.4 14.3 %copy-start.1 = (bf16[4096,384]{1,0:T(8,128)(2,1)S(1)}, bf16[4096,384]{1,0:T(8,128)(2,1)}, u32[]{:S(2)}) copy-start(bf16[4096,384]{1,0:T(8,128)(2,1)} %param.11) | copy-start | bytes 9437188
Sparse Core Ops, SparseCore 0:
  61.1 170.2 all-reduce.1
where the time goes:
time: 253 us
  waiting for transfers between devices  123 us (49%)
  matrix products  89.8 us (35%)
  local copies, waits for them, and re-layouts  25.3 us (10%)
  between operations  14.1 us (6%)
    psum x1, waiting for transfers between devices, step(): dx = lax.psum(term.astype(jnp.bfloat16), 'tp')  123 us
    unnamed x17, local copies, waits for them, and re-layouts  25.3 us
    dot_general x1, matrix products, step(): jnp.dot(d_up, w_up.T, preferred_element_type=jnp.float32)  23.1 us
    dot_general x1, matrix products, step(): d_hidden = jnp.dot(dy, w_down.T, preferred_element_type=jnp.float32)  16 us
    dot_general x1, matrix products, step(): jnp.dot(d_gate, w_gate.T, preferred_element_type=jnp.float32)  14.5 us
    dot_general x1, matrix products, step(): dw_up = jnp.dot(x.T, d_up, preferred_element_type=jnp.float32)  12.6 us
    dot_general x1, matrix products, step(): jnp.dot(hidden.astype(jnp.bfloat16).T, dy, preferred_element_type=jnp.flo...  12.2 us
    dot_general x1, matrix products, step(): dw_gate = jnp.dot(x.T, d_gate, preferred_element_type=jnp.float32)  11.5 us
  transfers between devices with their start and end apart: 1, of which 1 were waited for; matrix products, arithmetic and copies ran while one was open for 18% of the time, Pallas kernels for 0%

commit v1 on v0

v1 whole, which is shorter than its diff:
```python
import functools
import math

import jax
import jax.numpy as jnp
from jax import lax
from jax.experimental import pallas as pl
from jax.experimental.pallas import tpu as pltpu
from jax.sharding import PartitionSpec as P

F32, BF16 = jnp.float32, jnp.bfloat16
STEPS = 16
MIB = 1 << 20


def contract(a, b, ca, cb):
    return lax.dot_general(a, b, (((ca,), (cb,)), ((), ())), preferred_element_type=F32)


def kernel(
    side,
    x_hbm, dy_hbm, gate_hbm, up_hbm, wg_hbm, wu_hbm, wd_hbm,
    dx, dwg, dwu, dwd,
    wd_v, wc_v, gate_v, up_v, row_v, dc_v, ht_v, r1, r2, own, xcol_v, dycol_v,
    w_sem, row_sem, col_sem,
    free, pair_s, pair_r, one_s, one_r, two_s, two_r, ag2_s, ag2_r, ag1_s, ag1_r, agp_s, agp_r,
):
    rows, width = dx.shape
    f = wd_v.shape[0]
    half, hw = rows // 2, width // 2
    gr = half // side
    ur = gr // side
    cb = width // STEPS

    me = lax.axis_index("tp")
    c = lax.rem(me, 2)
    chip = lax.div(me, 2)
    cx, cy = lax.div(chip, side), lax.rem(chip, side)
    p = cx * (1 - c) + cy * c
    q = cy * (1 - c) + cx * c

    def wrap(v):
        return lax.rem(v + side, side)

    def device(pp, qq, cc):
        return {"tp": ((pp * (1 - cc) + qq * cc) * side + (qq * (1 - cc) + pp * cc)) * 2 + cc}

    partner = {"tp": chip * 2 + (1 - c)}
    p_dev = (device(wrap(p + 1), q, c), device(wrap(p - 1), q, c))
    q_dev = (device(p, wrap(q + 1), c), device(p, wrap(q - 1), c))
    offs = (2, 1, -1, 0)
    pg = [wrap(p + o) for o in offs]
    qg = [wrap(q + o) for o in offs]

    def row_of(cc, g, u):
        return pl.multiple_of(cc * half + g * gr + u * ur, ur)

    def remote(src, dst, s, r, dev):
        return pltpu.make_async_remote_copy(
            src_ref=src, dst_ref=dst, send_sem=s, recv_sem=r, device_id=dev, device_id_type=pl.DeviceIdType.MESH
        )

    sent = []

    def send(src, dst, s, r, dev):
        d = remote(src, dst, s, r, dev)
        d.start()
        sent.append(d)

    def arrived(ref, r):
        remote(ref, ref, r, r, partner).wait_recv()

    def lanes(h):
        return pl.ds(h * hw, hw)

    def release(k, devices):
        for d in sent:
            d.wait_send()
        sent.clear()
        for dev in devices:
            pl.semaphore_signal(free.at[k], inc=1, device_id=dev, device_id_type=pl.DeviceIdType.MESH)

    w_copies = [
        pltpu.make_async_copy(wd_hbm, wd_v, w_sem.at[0]),
        pltpu.make_async_copy(wg_hbm, wc_v.at[:, pl.ds(0, f)], w_sem.at[1]),
        pltpu.make_async_copy(wu_hbm, wc_v.at[:, pl.ds(f, f)], w_sem.at[2]),
    ]
    order = [(1 - c, qg[0]), (c, pg[0]), (1 - c, qg[1]), (1 - c, qg[2]), (c, pg[1]), (c, pg[2]), (1 - c, qg[3]), (c, pg[3])]

    def row_copies(i):
        at = pl.ds(row_of(*order[i], 0), gr)
        slot = i % 2
        return [
            pltpu.make_async_copy(dy_hbm.at[at, :], row_v.at[slot], row_sem.at[slot, 0]),
            pltpu.make_async_copy(gate_hbm.at[at, :], gate_v.at[slot], row_sem.at[slot, 1]),
            pltpu.make_async_copy(up_hbm.at[at, :], up_v.at[slot], row_sem.at[slot, 2]),
        ]

    def col_copies(i, slot):
        at = pl.ds(pl.multiple_of(i * cb, cb), cb)
        return [
            pltpu.make_async_copy(x_hbm.at[:, at], xcol_v.at[slot], col_sem.at[slot, 0]),
            pltpu.make_async_copy(dy_hbm.at[:, at], dycol_v.at[slot], col_sem.at[slot, 1]),
        ]

    w_copies[0].start()
    for d in row_copies(0):
        d.start()
    for d in w_copies[1:]:
        d.start()

    barrier = pltpu.get_barrier_semaphore()
    for dev in (partner, *p_dev, *q_dev):
        pl.semaphore_signal(barrier, inc=1, device_id=dev, device_id_type=pl.DeviceIdType.MESH)
    pl.semaphore_wait(barrier, 5)

    w_copies[0].wait()

    def hidden(i):
        slot = i % 2
        if i + 1 < len(order):
            for d in row_copies(i + 1):
                d.start()
        for d in row_copies(i):
            d.wait()
        dh = contract(row_v[slot], wd_v[...], 1, 1)
        g, u = gate_v[slot].astype(F32), up_v[slot].astype(F32)
        s = jax.nn.sigmoid(g)
        silu = g * s
        at = pl.ds(row_of(*order[i], 0), gr)
        dc_v[at, pl.ds(0, f)] = (dh * u * (s + silu * (1.0 - s))).astype(BF16)
        dc_v[at, pl.ds(f, f)] = (dh * silu).astype(BF16)
        ht_v[:, pl.ds(pl.multiple_of(row_of(*order[i], 0), gr), gr)] = (silu * u).astype(BF16).T

    tw = hw // 2

    def term(i, h, finish):
        at = pl.ds(row_of(*order[i], 0), gr)

        @pl.loop(0, hw // tw)
        def _(j):
            col = pl.ds(pl.multiple_of(h * hw + j * tw, tw), tw)
            finish(at, col, pl.ds(pl.multiple_of(j * tw, tw), tw), contract(dc_v[at, :], wc_v[col, :], 1, 1))

    def put(at, col, _, t):
        dx[at, col] = t.astype(BF16)

    def add(at, col, _, t):
        dx[at, col] = (t + dx[at, col].astype(F32)).astype(BF16)

    def add_from(ring):
        def finish(at, col, local, t):
            dx[at, col] = (t + dx[at, col].astype(F32) + ring[:, local].astype(F32)).astype(BF16)

        return finish

    def keep(at, col, _, t):
        own[:, col] = t + dx[at, col].astype(F32)

    def to_partner(i, k):
        for h in range(2):
            term(i, h, put)
            part = dx.at[pl.ds(row_of(*order[i], 0), gr), lanes(h)]
            send(part, part, pair_s.at[k, h], pair_r.at[k, h], partner)

    def from_partner(i, k, h):
        arrived(dx.at[pl.ds(row_of(*order[i], 0), gr), lanes(h)], pair_r.at[k, h])

    def dw_block(i):
        slot = lax.rem(i, 2)

        @pl.when(i + 1 < STEPS)
        def _():
            for d in col_copies(i + 1, 1 - slot):
                d.start()

        for d in col_copies(i, slot):
            d.wait()
        at = pl.ds(pl.multiple_of(i * cb, cb), cb)
        both = contract(xcol_v[slot], dc_v[...], 0, 0).astype(BF16)
        dwg[at, :] = both[:, :f]
        dwu[at, :] = both[:, f:]
        dwd[:, at] = jnp.dot(ht_v[...], dycol_v[slot], preferred_element_type=F32).astype(BF16)

    done = [0]

    def dw(n):
        lo = done[0]
        done[0] = min(STEPS, lo + n)
        pl.loop(lo, done[0])(dw_block)

    hidden(0)
    for d in w_copies[1:]:
        d.wait()
    to_partner(0, 0)
    hidden(1)
    at = pl.ds(row_of(c, pg[0], 0), gr)
    for h, way in ((1, 0), (0, 1)):
        from_partner(1, 0, h)
        term(1, h, add)
        send(dx.at[at, lanes(h)], r1.at[way, 0], one_s.at[way, 0], one_r.at[way, 0], p_dev[way])
    hidden(2)
    to_partner(2, 1)
    hidden(3)
    to_partner(3, 2)
    hidden(4)
    hidden(5)
    for i, k, h, way in ((4, 1, 0, 0), (5, 2, 1, 1)):
        from_partner(i, k, h)
        term(i, h, add)
        at = pl.ds(row_of(*order[i], 0), gr)
        send(dx.at[at, lanes(h)], r1.at[way, 1], one_s.at[way, 1], one_r.at[way, 1], p_dev[way])
    for d in col_copies(0, 0):
        d.start()
    for i, k, h, way in ((4, 1, 1, 0), (5, 2, 0, 1)):
        from_partner(i, k, h)
        arrived(r1.at[way, 0], one_r.at[way, 0])
        term(i, h, add_from(r1.at[way, 0]))
        for s in range(side):
            at = pl.ds(row_of(c, pg[k], qg[s]), ur)
            to = r1.at[way, 2, pl.ds(pl.multiple_of(qg[s] * ur, ur), ur)]
            send(dx.at[at, lanes(h)], to, one_s.at[way, 2 + s], one_r.at[way, 2 + s], p_dev[way])
    hidden(6)
    to_partner(6, 3)
    hidden(7)
    for h in range(2):
        from_partner(7, 3, h)
        term(7, h, keep)
    dw(2)
    for h in range(2):
        arrived(r1.at[h, 1], one_r.at[h, 1])
        own[:, lanes(h)] += r1[h, 1].astype(F32)
    dw(1)

    def unit(s):
        return pl.ds(pl.multiple_of(qg[s] * ur, ur), ur)

    def unit_dx(s):
        return pl.ds(row_of(c, p, qg[s]), ur)

    def close_one(s):
        for h, way in ((1, 0), (0, 1)):
            arrived(r1.at[way, 2, unit(s)], one_r.at[way, 2 + s])
            own[unit(s), lanes(h)] += r1[way, 2, unit(s)].astype(F32)

    def second(s, h, way, k):
        dx[unit_dx(s), lanes(h)] = own[unit(s), lanes(h)].astype(BF16)
        send(dx.at[unit_dx(s), lanes(h)], r2.at[way, k], two_s.at[way, k], two_r.at[way, k], q_dev[way])

    def add_two(s, h, way, k):
        arrived(r2.at[way, k], two_r.at[way, k])
        own[unit(s), lanes(h)] += r2[way, k].astype(F32)

    close_one(0)
    second(0, 1, 0, 0)
    second(0, 0, 1, 0)
    dw(1)
    close_one(1)
    second(1, 0, 0, 1)
    close_one(2)
    second(2, 1, 1, 1)
    dw(1)
    add_two(1, 1, 0, 0)
    second(1, 1, 0, 2)
    add_two(2, 0, 1, 0)
    second(2, 0, 1, 2)
    close_one(3)
    add_two(3, 0, 0, 1)
    add_two(3, 1, 1, 1)
    dw(1)
    release(0, (partner, *p_dev, *q_dev))
    add_two(3, 1, 0, 2)
    add_two(3, 0, 1, 2)
    dx[unit_dx(3), :] = own[unit(3), :].astype(BF16)

    uo = [q, wrap(q - 1), wrap(q + 1), wrap(q + 2)]
    go = [p, wrap(p - 1), wrap(p + 1), wrap(p + 2)]

    def piece(j, s, h=None):
        at = pl.ds(row_of(c, go[j], uo[s]), ur)
        return dx.at[at, :] if h is None else dx.at[at, lanes(h)]

    def spread(s):
        for way in range(2):
            send(piece(0, s), piece(0, s), ag1_s.at[way, s], ag1_r.at[way, s], p_dev[way])

    def share(j, s):
        send(piece(j, s), piece(j, s), agp_s.at[j, s], agp_r.at[j, s], partner)

    def relay(s):
        for way, h in ((0, 1), (1, 0)):
            arrived(piece(1 + way, s), ag1_r.at[way, s])
            send(piece(1 + way, s, h), piece(1 + way, s, h), ag1_s.at[2 + way, s], ag1_r.at[2 + way, s], p_dev[way])
            share(1 + way, s)

    def finish(s):
        for way, h in ((0, 1), (1, 0)):
            arrived(piece(3, s, h), ag1_r.at[2 + way, s])
        share(3, s)

    pl.semaphore_wait(free.at[0], 5)
    for way in range(2):
        send(piece(0, 0), piece(0, 0), ag2_s.at[way], ag2_r.at[way], q_dev[way])
    spread(0)
    share(0, 0)
    dw(2)
    for way, h in ((0, 1), (1, 0)):
        arrived(piece(0, 1 + way), ag2_r.at[way])
        send(piece(0, 1 + way, h), piece(0, 1 + way, h), ag2_s.at[2 + way], ag2_r.at[2 + way], q_dev[way])
        spread(1 + way)
        share(0, 1 + way)
    relay(0)
    dw(1)
    for way, h in ((0, 1), (1, 0)):
        arrived(piece(0, 3, h), ag2_r.at[2 + way])
    spread(3)
    share(0, 3)
    dw(2)
    relay(1)
    finish(0)
    dw(2)
    relay(2)
    finish(1)
    dw(STEPS)
    relay(3)
    finish(2)
    finish(3)
    for j in range(side):
        for s in range(side):
            arrived(piece(j, s), agp_r.at[j, s])
    for d in sent:
        d.wait_send()


def put_out(*refs):
    copies = [pltpu.make_async_copy(refs[i], refs[4 + i], refs[8].at[i]) for i in range(4)]
    for d in copies:
        d.start()
    for d in copies:
        d.wait()


def solution(mesh):
    tp = mesh.shape["tp"]
    side = math.isqrt(tp // 2)
    assert side == 4 and 2 * side * side == tp

    def step(x, dy, gate, up, w_gate, w_up, w_down):
        rows, width = x.shape
        f = gate.shape[1]
        gr, ur, cb, hw = rows // 8, rows // 32, width // STEPS, width // 2
        dma = pltpu.SemaphoreType.DMA
        out = lambda *s: pltpu.VMEM(s, BF16)
        flops = 12 * rows * width * f
        held = pl.pallas_call(
            functools.partial(kernel, side),
            out_shape=(out(rows, width), out(width, f), out(width, f), out(f, width)),
            in_specs=[pl.BlockSpec(memory_space=pl.ANY)] * 7,
            out_specs=[pl.BlockSpec(memory_space=pltpu.VMEM)] * 4,
            scratch_shapes=[
                pltpu.VMEM((f, width), BF16),
                pltpu.VMEM((width, 2 * f), BF16),
                pltpu.VMEM((2, gr, f), BF16),
                pltpu.VMEM((2, gr, f), BF16),
                pltpu.VMEM((2, gr, width), BF16),
                pltpu.VMEM((rows, 2 * f), BF16),
                pltpu.VMEM((f, rows), BF16),
                pltpu.VMEM((2, 3, gr, hw), BF16),
                pltpu.VMEM((2, 3, ur, hw), BF16),
                pltpu.VMEM((gr, width), F32),
                pltpu.VMEM((2, rows, cb), BF16),
                pltpu.VMEM((2, rows, cb), BF16),
                dma((3,)),
                dma((2, 3)),
                dma((2, 2)),
                pltpu.SemaphoreType.REGULAR((1,)),
                dma((4, 2)), dma((4, 2)),
                dma((2, 6)), dma((2, 6)),
                dma((2, 3)), dma((2, 3)),
                dma((4,)), dma((4,)),
                dma((4, 4)), dma((4, 4)),
                dma((4, 4)), dma((4, 4)),
            ],
            compiler_params=pltpu.CompilerParams(
                collective_id=0, has_side_effects=True, vmem_limit_bytes=VMEM_LIMIT
            ),
            cost_estimate=pl.CostEstimate(flops=flops, bytes_accessed=80 * MIB, transcendentals=rows * f),
        )(x, dy, gate, up, w_gate, w_up, w_down)
        return pl.pallas_call(
            put_out,
            out_shape=tuple(jax.ShapeDtypeStruct(h.shape, h.dtype) for h in held),
            in_specs=[pl.BlockSpec(memory_space=pltpu.VMEM)] * 4,
            out_specs=[pl.BlockSpec(memory_space=pltpu.HBM)] * 4,
            scratch_shapes=[dma((4,))],
            compiler_params=pltpu.CompilerParams(vmem_limit_bytes=2 * MIB),
        )(*held)

    tokens, columns, rows = P("dp", None), P(None, "tp"), P("tp", None)
    return jax.shard_map(
        step,
        mesh=mesh,
        in_specs=(tokens, tokens, P("dp", "tp"), P("dp", "tp"), columns, columns, rows),
        out_specs=(tokens, P("dp", "tp"), P("dp", "tp"), P(("dp", "tp"), None)),
        check_vma=False,
    )


VMEM_LIMIT = 37 * MIB
```

time: 253 us -> 129 us (0.51)
  Pallas kernels: 0 us -> 128 us
  waiting for transfers between devices: 123 us -> 0 us
  matrix products: 89.8 us -> 0 us
  local copies, waits for them, and re-layouts: 25.3 us -> 0 us
  between operations: 14.1 us -> 0.82 us
    pallas_call x0 -> x2, Pallas kernels: none -> 128 us  [the longest x1 119 us: step(): pl.pallas_call(functools.partial(kernel, side), out_shape=(out(rows, widt...]
    psum x1 -> x0, waiting for transfers between devices: 123 us -> none  [step(): dx = lax.psum(term.astype(jnp.bfloat16), 'tp')]
    dot_general x6 -> x0, matrix products: 89.8 us -> none  [the longest x1 23.1 us: step(): jnp.dot(d_up, w_up.T, preferred_element_type=jnp.float32)]
    unnamed x17 -> x0, local copies, waits for them, and re-layouts: 25.3 us -> none
  transfers between devices with their start and end apart: 1 -> 0, of which waited for: 1 -> 0; matrix products, arithmetic and copies ran while one was open for 18% -> 0% of each run, Pallas kernels for 0% -> 0%
where the time goes in v1:
time: 129 us
  Pallas kernels  128 us (99%)
    pallas_call x1, Pallas kernels, step(): pl.pallas_call(functools.partial(kernel, side), out_shape=(out(rows, widt...  119 us
    pallas_call x1, Pallas kernels, step(): pl.pallas_call(put_out, out_shape=tuple((jax.ShapeDtypeStruct(h.shape, h....  9.11 us

profile of v1, /device:TPU:97, one launch (start us, length us, event | category | flops | bytes accessed | tf_op | source)
XLA Modules:
  0.0 128.8 jit_solution(13683309549629195467)
XLA Ops:
  0.6 118.8 %shard_map.102 = (bf16[2048,4096]{1,0:T(8,128)(2,1)S(1)}, bf16[4096,384]{1,0:T(8,128)(2,1)S(1)}, bf16[4096,384]{1,0:T(8,128)(2,1)S(1)}, bf16[384,4096]{1,0:T(8,128)(2,1)S(1)}) custom-call(bf16[2048,4096]{1,0:T(8,128)(2,1)} %x_hbm.1, bf16[2048,4096]{1,0:T(8,128)(2,1)} %dy_hbm.1, bf16[2048,384]{1,0:T(8,128)(2,1)} %gate_hbm.1, bf16[2048,384]{1,0:T(8,128)(2,1)} %up_hbm.1, ...), custom_call_target="tpu_custom_call" | custom-call | flops 38654705664 | bytes 83886080 | tf_op jit(solution)/shard_map/pallas_call | solution.py:355
  119.5 9.1 %shard_map.103 = (bf16[2048,4096]{1,0:T(8,128)(2,1)}, bf16[4096,384]{1,0:T(8,128)(2,1)}, bf16[4096,384]{1,0:T(8,128)(2,1)}, bf16[384,4096]{1,0:T(8,128)(2,1)}) custom-call(bf16[2048,4096]{1,0:T(8,128)(2,1)S(1)} %get-tuple-element.8.refs_0_, bf16[4096,384]{1,0:T(8,128)(2,1)S(1)} %get-tuple-element.9.refs_1_, bf16[4096,384]{1,0:T(8,128)(2,1)S(1)} %get-tuple-element.10.refs_2_, ...), custom_call_target="tpu_custom_call" | custom-call | tf_op jit(solution)/shard_map/pallas_call | solution.py:389

commit v2 on v1

v2 whole, which is shorter than its diff:
```python
import functools
import math

import jax
import jax.numpy as jnp
from jax import lax
from jax.experimental import pallas as pl
from jax.experimental.pallas import tpu as pltpu
from jax.sharding import PartitionSpec as P

F32, BF16 = jnp.float32, jnp.bfloat16
STEPS = 16
PARTS = 4
MIB = 1 << 20


def contract(a, b, ca, cb):
    return lax.dot_general(a, b, (((ca,), (cb,)), ((), ())), preferred_element_type=F32)


def kernel(
    side,
    x_hbm, dy_hbm, gate_hbm, up_hbm, wg_hbm, wu_hbm, wd_hbm,
    dx, dwg, dwu, dwd,
    wd_v, wc_v, gate_v, up_v, row_v, dc_v, ht_v, r1, r2, own, xcol_v, dycol_v,
    w_sem, row_sem, col_sem,
    free, pair_s, pair_r, one_s, one_r, two_s, two_r, ag2_s, ag2_r, ag1_s, ag1_r, agp_s, agp_r,
):
    rows, width = dx.shape
    f = wd_v.shape[0]
    half, hw = rows // 2, width // 2
    gr = half // side
    ur = gr // side
    cb = width // STEPS

    me = lax.axis_index("tp")
    c = lax.rem(me, 2)
    chip = lax.div(me, 2)
    cx, cy = lax.div(chip, side), lax.rem(chip, side)
    p = cx * (1 - c) + cy * c
    q = cy * (1 - c) + cx * c

    def wrap(v):
        return lax.rem(v + side, side)

    def device(pp, qq, cc):
        return {"tp": ((pp * (1 - cc) + qq * cc) * side + (qq * (1 - cc) + pp * cc)) * 2 + cc}

    partner = {"tp": chip * 2 + (1 - c)}
    p_dev = (device(wrap(p + 1), q, c), device(wrap(p - 1), q, c))
    q_dev = (device(p, wrap(q + 1), c), device(p, wrap(q - 1), c))
    offs = (2, 1, -1, 0)
    pg = [wrap(p + o) for o in offs]
    qg = [wrap(q + o) for o in offs]

    def row_of(cc, g, u):
        return pl.multiple_of(cc * half + g * gr + u * ur, ur)

    def remote(src, dst, s, r, dev):
        return pltpu.make_async_remote_copy(
            src_ref=src, dst_ref=dst, send_sem=s, recv_sem=r, device_id=dev, device_id_type=pl.DeviceIdType.MESH
        )

    def arrived(ref, r):
        remote(ref, ref, r, r, partner).wait_recv()

    def left(ref, s):
        remote(ref, ref, s, s, partner).wait_send()

    qw = width // 4

    def lanes(w, h):
        return pl.ds(pl.multiple_of(w * hw + h * qw, qw), qw)

    def whole(w):
        return pl.ds(w * hw, hw)

    w_copies = [
        pltpu.make_async_copy(wd_hbm, wd_v, w_sem.at[0]),
        pltpu.make_async_copy(wg_hbm, wc_v.at[:, pl.ds(0, f)], w_sem.at[1]),
        pltpu.make_async_copy(wu_hbm, wc_v.at[:, pl.ds(f, f)], w_sem.at[2]),
    ]
    order = [(1 - c, qg[0]), (c, pg[0]), (1 - c, qg[1]), (1 - c, qg[2]), (c, pg[1]), (c, pg[2]), (1 - c, qg[3]), (c, pg[3])]

    def row_copies(i):
        at = pl.ds(row_of(*order[i], 0), gr)
        slot = i % 2
        return [
            pltpu.make_async_copy(dy_hbm.at[at, :], row_v.at[slot], row_sem.at[slot, 0]),
            pltpu.make_async_copy(gate_hbm.at[at, :], gate_v.at[slot], row_sem.at[slot, 1]),
            pltpu.make_async_copy(up_hbm.at[at, :], up_v.at[slot], row_sem.at[slot, 2]),
        ]

    def col_copies(i, slot):
        at = pl.ds(pl.multiple_of(i * cb, cb), cb)
        return [
            pltpu.make_async_copy(x_hbm.at[:, at], xcol_v.at[slot], col_sem.at[slot, 0]),
            pltpu.make_async_copy(dy_hbm.at[:, at], dycol_v.at[slot], col_sem.at[slot, 1]),
        ]

    w_copies[0].start()
    for d in row_copies(0):
        d.start()
    for d in w_copies[1:]:
        d.start()

    barrier = pltpu.get_barrier_semaphore()
    for dev in (partner, *p_dev, *q_dev):
        pl.semaphore_signal(barrier, inc=1, device_id=dev, device_id_type=pl.DeviceIdType.MESH)

    w_copies[0].wait()

    def hidden(i):
        slot = i % 2
        if i + 1 < len(order):
            for d in row_copies(i + 1):
                d.start()
        for d in row_copies(i):
            d.wait()
        dh = contract(row_v[slot], wd_v[...], 1, 1)
        g, u = gate_v[slot].astype(F32), up_v[slot].astype(F32)
        s = jax.nn.sigmoid(g)
        silu = g * s
        at = pl.ds(row_of(*order[i], 0), gr)
        dc_v[at, pl.ds(0, f)] = (dh * u * (s + silu * (1.0 - s))).astype(BF16)
        dc_v[at, pl.ds(f, f)] = (dh * silu).astype(BF16)
        ht_v[:, pl.ds(pl.multiple_of(row_of(*order[i], 0), gr), gr)] = (silu * u).astype(BF16).T

    def term(row, w, h):
        return contract(dc_v[pl.ds(row, gr), :], wc_v[lanes(w, h), :], 1, 1)

    def piece_of(row, w, h):
        return dx.at[pl.ds(row, gr), lanes(w, h)]

    def to_partner(k, w):
        row = row_of(1 - c, qg[k], 0)

        @pl.loop(0, 2)
        def _(h):
            part = piece_of(row, w, h)
            part[...] = term(row, w, h).astype(BF16)
            remote(part, part, pair_s.at[w, k, h], pair_r.at[w, k, h], partner).start()

    def with_partner(k, w, h, row):
        part = piece_of(row, w, h)
        arrived(part, pair_r.at[w, k, h])
        return part, term(row, w, h) + part[...].astype(F32)

    def p_at(way):
        return {"tp": p_dev[0]["tp"] * (1 - way) + p_dev[1]["tp"] * way}

    def first_far(w):
        row = row_of(c, pg[0], 0)

        @pl.loop(0, 2)
        def _(way):
            part, t = with_partner(0, w, 1 - way, row)
            part[...] = t.astype(BF16)
            remote(part, r1.at[w, way, 0], one_s.at[w, way, 0], one_r.at[w, way, 0], p_at(way)).start()

    def first_near(w):
        @pl.loop(0, 2)
        def _(way):
            row = row_of(c, pg[1] * (1 - way) + pg[2] * way, 0)
            part, t = with_partner(1 + way, w, way, row)
            part[...] = t.astype(BF16)
            remote(part, r1.at[w, way, 1], one_s.at[w, way, 1], one_r.at[w, way, 1], p_at(way)).start()

    def first_joined(w):
        @pl.loop(0, 2)
        def _(way):
            row = row_of(c, pg[1] * (1 - way) + pg[2] * way, 0)
            part, t = with_partner(1 + way, w, 1 - way, row)
            arrived(r1.at[w, way, 0], one_r.at[w, way, 0])
            part[...] = (t + r1[w, way, 0].astype(F32)).astype(BF16)
            for s in range(side):
                at = unit(s)
                to = r1.at[w, way, 2, at]
                remote(part.at[at], to, one_s.at[w, way, 2 + s], one_r.at[w, way, 2 + s], p_at(way)).start()

    def first_own(w):
        @pl.loop(0, 2)
        def _(h):
            _, t = with_partner(3, w, h, row_of(c, pg[3], 0))
            own[:, lanes(w, h)] = t

    def unit(s):
        return pl.ds(pl.multiple_of(qg[s] * ur, ur), ur)

    def dw_block(i):
        slot = lax.rem(i, 2)

        @pl.when(i + 1 < STEPS)
        def _():
            for d in col_copies(i + 1, 1 - slot):
                d.start()

        for d in col_copies(i, slot):
            d.wait()
        at = pl.ds(pl.multiple_of(i * cb, cb), cb)
        both = contract(xcol_v[slot], dc_v[...], 0, 0).astype(BF16)
        dwg[at, :] = both[:, :f]
        dwu[at, :] = both[:, f:]
        dwd[:, at] = jnp.dot(ht_v[...], dycol_v[slot], preferred_element_type=F32).astype(BF16)

    done = [0]

    def dw(n):
        lo = done[0]
        done[0] = min(STEPS, lo + n)
        pl.loop(lo, done[0])(dw_block)

    def first_in(w):
        for h in range(2):
            arrived(r1.at[w, h, 1], one_r.at[w, h, 1])
            own[:, lanes(w, h)] += r1[w, h, 1].astype(F32)

    def unit_dx(s):
        return pl.ds(row_of(c, p, qg[s]), ur)

    def close_one(s, w):
        for h, way in ((1, 0), (0, 1)):
            arrived(r1.at[w, way, 2, unit(s)], one_r.at[w, way, 2 + s])
            own[unit(s), lanes(w, h)] += r1[w, way, 2, unit(s)].astype(F32)

    def second(s, w, h, way, k):
        part = dx.at[unit_dx(s), lanes(w, h)]
        part[...] = own[unit(s), lanes(w, h)].astype(BF16)
        remote(part, r2.at[w, way, k], two_s.at[w, way, k], two_r.at[w, way, k], q_dev[way]).start()

    def add_two(s, w, h, way, k):
        arrived(r2.at[w, way, k], two_r.at[w, way, k])
        own[unit(s), lanes(w, h)] += r2[w, way, k].astype(F32)

    def second_far(w):
        close_one(0, w)
        second(0, w, 1, 0, 0)
        second(0, w, 0, 1, 0)

    def second_near(w):
        close_one(1, w)
        second(1, w, 0, 0, 1)
        close_one(2, w)
        second(2, w, 1, 1, 1)

    def second_joined(w):
        add_two(1, w, 1, 0, 0)
        second(1, w, 1, 0, 2)
        add_two(2, w, 0, 1, 0)
        second(2, w, 0, 1, 2)

    def second_own(w):
        close_one(3, w)
        add_two(3, w, 0, 0, 1)
        add_two(3, w, 1, 1, 1)

    def close(w):
        add_two(3, w, 1, 0, 2)
        add_two(3, w, 0, 1, 2)
        dx[unit_dx(3), whole(w)] = own[unit(3), whole(w)].astype(BF16)

    def release(w):
        for k in range(side):
            for h in range(2):
                left(piece_of(row_of(1 - c, qg[k], 0), w, h), pair_s.at[w, k, h])
        for way in range(2):
            for k in range(2):
                left(r1.at[w, way, k], one_s.at[w, way, k])
            for s in range(side):
                left(r1.at[w, way, 2, unit(s)], one_s.at[w, way, 2 + s])
            for k in range(3):
                left(r2.at[w, way, k], two_s.at[w, way, k])
        for dev in (partner, *p_dev, *q_dev):
            pl.semaphore_signal(free.at[w], inc=1, device_id=dev, device_id_type=pl.DeviceIdType.MESH)

    uo = [q, wrap(q - 1), wrap(q + 1), wrap(q + 2)]
    go = [p, wrap(p - 1), wrap(p + 1), wrap(p + 2)]
    sent = []

    def send(src, s, r, dev):
        d = remote(src, src, s, r, dev)
        d.start()
        sent.append(d)

    def piece(j, s, w, h=None):
        return dx.at[pl.ds(row_of(c, go[j], uo[s]), ur), whole(w) if h is None else lanes(w, h)]

    def spread(s, w):
        for way in range(2):
            send(piece(0, s, w), ag1_s.at[w, way, s], ag1_r.at[w, way, s], p_dev[way])

    def share(j, s, w):
        send(piece(j, s, w), agp_s.at[w, j, s], agp_r.at[w, j, s], partner)

    def open_gather(w):
        pl.semaphore_wait(free.at[w], 5)
        for way in range(2):
            send(piece(0, 0, w), ag2_s.at[w, way], ag2_r.at[w, way], q_dev[way])
        spread(0, w)
        share(0, 0, w)

    def gather_near(w):
        for way, h in ((0, 1), (1, 0)):
            arrived(piece(0, 1 + way, w), ag2_r.at[w, way])
            send(piece(0, 1 + way, w, h), ag2_s.at[w, 2 + way], ag2_r.at[w, 2 + way], q_dev[way])
            spread(1 + way, w)
            share(0, 1 + way, w)

    def gather_far(w):
        for way, h in ((0, 1), (1, 0)):
            arrived(piece(0, 3, w, h), ag2_r.at[w, 2 + way])
        spread(3, w)
        share(0, 3, w)

    def relay(s, w):
        for way, h in ((0, 1), (1, 0)):
            arrived(piece(1 + way, s, w), ag1_r.at[w, way, s])
            send(piece(1 + way, s, w, h), ag1_s.at[w, 2 + way, s], ag1_r.at[w, 2 + way, s], p_dev[way])
            share(1 + way, s, w)

    def finish(s, w):
        for way, h in ((0, 1), (1, 0)):
            arrived(piece(3, s, w, h), ag1_r.at[w, 2 + way, s])
        share(3, s, w)

    hidden(0)
    for d in w_copies[1:]:
        d.wait()
    pl.semaphore_wait(barrier, 5)
    to_partner(0, 0)
    hidden(1)
    first_far(0)
    hidden(2)
    to_partner(1, 0)
    hidden(3)
    to_partner(2, 0)
    hidden(4)
    hidden(5)
    first_near(0)
    to_partner(0, 1)
    first_joined(0)
    hidden(6)
    to_partner(3, 0)
    hidden(7)
    for d in col_copies(0, 0):
        d.start()
    first_own(0)
    first_far(1)
    to_partner(1, 1)
    to_partner(2, 1)
    first_near(1)
    first_in(0)
    second_far(0)
    to_partner(3, 1)
    first_own(1)
    second_near(0)
    dw(2)
    second_joined(0)
    second_own(0)
    dw(2)
    first_joined(1)
    close(0)
    release(0)
    dw(1)
    open_gather(0)
    first_in(1)
    dw(2)
    second_far(1)
    second_near(1)
    gather_near(0)
    second_joined(1)
    relay(0, 0)
    second_own(1)
    gather_far(0)
    close(1)
    release(1)
    dw(2)
    open_gather(1)
    relay(1, 0)
    finish(0, 0)
    relay(2, 0)
    dw(2)
    gather_near(1)
    finish(1, 0)
    relay(3, 0)
    finish(2, 0)
    relay(0, 1)
    finish(3, 0)
    dw(2)
    gather_far(1)
    relay(1, 1)
    finish(0, 1)
    dw(STEPS)
    relay(2, 1)
    finish(1, 1)
    relay(3, 1)
    finish(2, 1)
    finish(3, 1)
    for w in range(2):
        for j in range(side):
            for s in range(side):
                arrived(piece(j, s, w), agp_r.at[w, j, s])
    for d in sent:
        d.wait_send()


def put_out(*refs):
    copies = []
    for i in range(4):
        rows = refs[i].shape[0] // PARTS
        for k in range(PARTS):
            at = pl.ds(k * rows, rows)
            copies.append(pltpu.make_async_copy(refs[i].at[at], refs[4 + i].at[at], refs[8].at[i, k]))
    for d in copies:
        d.start()
    for d in copies:
        d.wait()


def solution(mesh):
    tp = mesh.shape["tp"]
    side = math.isqrt(tp // 2)
    assert side == 4 and 2 * side * side == tp

    def step(x, dy, gate, up, w_gate, w_up, w_down):
        rows, width = x.shape
        f = gate.shape[1]
        gr, ur, cb, qw = rows // 8, rows // 32, width // STEPS, width // 4
        dma = pltpu.SemaphoreType.DMA
        out = lambda *s: pltpu.VMEM(s, BF16)
        flops = 12 * rows * width * f
        held = pl.pallas_call(
            functools.partial(kernel, side),
            out_shape=(out(rows, width), out(width, f), out(width, f), out(f, width)),
            in_specs=[pl.BlockSpec(memory_space=pl.ANY)] * 7,
            out_specs=[pl.BlockSpec(memory_space=pltpu.VMEM)] * 4,
            scratch_shapes=[
                pltpu.VMEM((f, width), BF16),
                pltpu.VMEM((width, 2 * f), BF16),
                pltpu.VMEM((2, gr, f), BF16),
                pltpu.VMEM((2, gr, f), BF16),
                pltpu.VMEM((2, gr, width), BF16),
                pltpu.VMEM((rows, 2 * f), BF16),
                pltpu.VMEM((f, rows), BF16),
                pltpu.VMEM((2, 2, 3, gr, qw), BF16),
                pltpu.VMEM((2, 2, 3, ur, qw), BF16),
                pltpu.VMEM((gr, width), F32),
                pltpu.VMEM((2, rows, cb), BF16),
                pltpu.VMEM((2, rows, cb), BF16),
                dma((3,)),
                dma((2, 3)),
                dma((2, 2)),
                pltpu.SemaphoreType.REGULAR((2,)),
                dma((2, 4, 2)), dma((2, 4, 2)),
                dma((2, 2, 6)), dma((2, 2, 6)),
                dma((2, 2, 3)), dma((2, 2, 3)),
                dma((2, 4)), dma((2, 4)),
                dma((2, 4, 4)), dma((2, 4, 4)),
                dma((2, 4, 4)), dma((2, 4, 4)),
            ],
            compiler_params=pltpu.CompilerParams(
                collective_id=0, has_side_effects=True, vmem_limit_bytes=VMEM_LIMIT
            ),
            cost_estimate=pl.CostEstimate(flops=flops, bytes_accessed=80 * MIB, transcendentals=rows * f),
        )(x, dy, gate, up, w_gate, w_up, w_down)
        return pl.pallas_call(
            put_out,
            out_shape=tuple(jax.ShapeDtypeStruct(h.shape, h.dtype) for h in held),
            in_specs=[pl.BlockSpec(memory_space=pltpu.VMEM)] * 4,
            out_specs=[pl.BlockSpec(memory_space=pltpu.HBM)] * 4,
            scratch_shapes=[dma((4, PARTS))],
            compiler_params=pltpu.CompilerParams(vmem_limit_bytes=2 * MIB),
        )(*held)

    tokens, columns, rows = P("dp", None), P(None, "tp"), P("tp", None)
    return jax.shard_map(
        step,
        mesh=mesh,
        in_specs=(tokens, tokens, P("dp", "tp"), P("dp", "tp"), columns, columns, rows),
        out_specs=(tokens, P("dp", "tp"), P("dp", "tp"), P(("dp", "tp"), None)),
        check_vma=False,
    )


VMEM_LIMIT = 37 * MIB
```

time: 129 us -> 127 us (0.984)
  Pallas kernels: 128 us -> 126 us
    pallas_call x1, Pallas kernels: 119 us -> 117 us  [step(): pl.pallas_call(functools.partial(kernel, side), out_shape=(out(rows, widt...]
where the time goes in v2:
time: 127 us
  Pallas kernels  126 us (99%)
    pallas_call x1, Pallas kernels, step(): pl.pallas_call(functools.partial(kernel, side), out_shape=(out(rows, widt...  117 us
    pallas_call x1, Pallas kernels, step(): pl.pallas_call(put_out, out_shape=tuple((jax.ShapeDtypeStruct(h.shape, h....  8.79 us

profile of v2, /device:TPU:97, one launch (start us, length us, event | category | flops | bytes accessed | tf_op | source)
XLA Modules:
  0.0 126.9 jit_solution(8759297112018443960)
XLA Ops:
  0.6 117.2 %shard_map.102 = (bf16[2048,4096]{1,0:T(8,128)(2,1)S(1)}, bf16[4096,384]{1,0:T(8,128)(2,1)S(1)}, bf16[4096,384]{1,0:T(8,128)(2,1)S(1)}, bf16[384,4096]{1,0:T(8,128)(2,1)S(1)}) custom-call(bf16[2048,4096]{1,0:T(8,128)(2,1)} %x_hbm.1, bf16[2048,4096]{1,0:T(8,128)(2,1)} %dy_hbm.1, bf16[2048,384]{1,0:T(8,128)(2,1)} %gate_hbm.1, bf16[2048,384]{1,0:T(8,128)(2,1)} %up_hbm.1, ...), custom_call_target="tpu_custom_call" | custom-call | flops 38654705664 | bytes 83886080 | tf_op jit(solution)/shard_map/pallas_call | solution.py:432
  117.9 8.8 %shard_map.103 = (bf16[2048,4096]{1,0:T(8,128)(2,1)}, bf16[4096,384]{1,0:T(8,128)(2,1)}, bf16[4096,384]{1,0:T(8,128)(2,1)}, bf16[384,4096]{1,0:T(8,128)(2,1)}) custom-call(bf16[2048,4096]{1,0:T(8,128)(2,1)S(1)} %get-tuple-element.8.refs_0_, bf16[4096,384]{1,0:T(8,128)(2,1)S(1)} %get-tuple-element.9.refs_1_, bf16[4096,384]{1,0:T(8,128)(2,1)S(1)} %get-tuple-element.10.refs_2_, ...), custom_call_target="tpu_custom_call" | custom-call | tf_op jit(solution)/shard_map/pallas_call | solution.py:466

commit v3 on v2

--- a/solution.py
+++ b/solution.py
@@ -75,11 +75,13 @@
     def whole(w):
         return pl.ds(w * hw, hw)
 
-    w_copies = [
-        pltpu.make_async_copy(wd_hbm, wd_v, w_sem.at[0]),
-        pltpu.make_async_copy(wg_hbm, wc_v.at[:, pl.ds(0, f)], w_sem.at[1]),
-        pltpu.make_async_copy(wu_hbm, wc_v.at[:, pl.ds(f, f)], w_sem.at[2]),
-    ]
+    w_copies = [pltpu.make_async_copy(wd_hbm, wd_v, w_sem.at[0])]
+    for w in range(2):
+        at = pl.ds(w * hw, hw)
+        w_copies += [
+            pltpu.make_async_copy(wg_hbm.at[at, :], wc_v.at[at, pl.ds(0, f)], w_sem.at[1 + 2 * w]),
+            pltpu.make_async_copy(wu_hbm.at[at, :], wc_v.at[at, pl.ds(f, f)], w_sem.at[2 + 2 * w]),
+        ]
     order = [(1 - c, qg[0]), (c, pg[0]), (1 - c, qg[1]), (1 - c, qg[2]), (c, pg[1]), (c, pg[2]), (1 - c, qg[3]), (c, pg[3])]
 
     def row_copies(i):
@@ -101,7 +103,7 @@
     w_copies[0].start()
     for d in row_copies(0):
         d.start()
-    for d in w_copies[1:]:
+    for d in w_copies[1:3]:
         d.start()
 
     barrier = pltpu.get_barrier_semaphore()
@@ -153,8 +155,9 @@
         row = row_of(c, pg[0], 0)
 
         @pl.loop(0, 2)
-        def _(way):
-            part, t = with_partner(0, w, 1 - way, row)
+        def _(h):
+            way = 1 - h
+            part, t = with_partner(0, w, h, row)
             part[...] = t.astype(BF16)
             remote(part, r1.at[w, way, 0], one_s.at[w, way, 0], one_r.at[w, way, 0], p_at(way)).start()
 
@@ -243,11 +246,9 @@
         close_one(2, w)
         second(2, w, 1, 1, 1)
 
-    def second_joined(w):
-        add_two(1, w, 1, 0, 0)
-        second(1, w, 1, 0, 2)
-        add_two(2, w, 0, 1, 0)
-        second(2, w, 0, 1, 2)
+    def second_joined(way, w):
+        add_two(1 + way, w, 1 - way, way, 0)
+        second(1 + way, w, 1 - way, way, 2)
 
     def second_own(w):
         close_one(3, w)
@@ -299,12 +300,11 @@
         spread(0, w)
         share(0, 0, w)
 
-    def gather_near(w):
-        for way, h in ((0, 1), (1, 0)):
-            arrived(piece(0, 1 + way, w), ag2_r.at[w, way])
-            send(piece(0, 1 + way, w, h), ag2_s.at[w, 2 + way], ag2_r.at[w, 2 + way], q_dev[way])
-            spread(1 + way, w)
-            share(0, 1 + way, w)
+    def gather_near(way, w):
+        arrived(piece(0, 1 + way, w), ag2_r.at[w, way])
+        send(piece(0, 1 + way, w, 1 - way), ag2_s.at[w, 2 + way], ag2_r.at[w, 2 + way], q_dev[way])
+        spread(1 + way, w)
+        share(0, 1 + way, w)
 
     def gather_far(w):
         for way, h in ((0, 1), (1, 0)):
@@ -312,11 +312,10 @@
         spread(3, w)
         share(0, 3, w)
 
-    def relay(s, w):
-        for way, h in ((0, 1), (1, 0)):
-            arrived(piece(1 + way, s, w), ag1_r.at[w, way, s])
-            send(piece(1 + way, s, w, h), ag1_s.at[w, 2 + way, s], ag1_r.at[w, 2 + way, s], p_dev[way])
-            share(1 + way, s, w)
+    def relay(way, s, w):
+        arrived(piece(1 + way, s, w), ag1_r.at[w, way, s])
+        send(piece(1 + way, s, w, 1 - way), ag1_s.at[w, 2 + way, s], ag1_r.at[w, 2 + way, s], p_dev[way])
+        share(1 + way, s, w)
 
     def finish(s, w):
         for way, h in ((0, 1), (1, 0)):
@@ -324,7 +323,9 @@
         share(3, s, w)
 
     hidden(0)
-    for d in w_copies[1:]:
+    for d in w_copies[3:]:
+        d.start()
+    for d in w_copies[1:3]:
         d.wait()
     pl.semaphore_wait(barrier, 5)
     to_partner(0, 0)
@@ -336,64 +337,77 @@
     to_partner(2, 0)
     hidden(4)
     hidden(5)
+    hidden(6)
     first_near(0)
-    to_partner(0, 1)
-    first_joined(0)
-    hidden(6)
     to_partner(3, 0)
     hidden(7)
     for d in col_copies(0, 0):
         d.start()
+    for d in w_copies[3:]:
+        d.wait()
+    to_partner(0, 1)
+    first_joined(0)
     first_own(0)
+    to_partner(1, 1)
     first_far(1)
-    to_partner(1, 1)
     to_partner(2, 1)
+    to_partner(3, 1)
+    dw(1)
+    first_in(0)
+    dw(1)
+    second_far(0)
     first_near(1)
-    first_in(0)
-    second_far(0)
-    to_partner(3, 1)
     first_own(1)
     second_near(0)
+    dw(3)
+    second_joined(0, 0)
+    second_joined(1, 0)
     dw(2)
-    second_joined(0)
     second_own(0)
-    dw(2)
-    first_joined(1)
+    dw(3)
     close(0)
     release(0)
     dw(1)
     open_gather(0)
+    first_joined(1)
+    dw(5)
     first_in(1)
-    dw(2)
+    gather_near(0, 0)
+    gather_near(1, 0)
+    relay(0, 0, 0)
+    relay(1, 0, 0)
+    gather_far(0)
     second_far(1)
     second_near(1)
-    gather_near(0)
-    second_joined(1)
-    relay(0, 0)
+    second_joined(0, 1)
+    second_joined(1, 1)
     second_own(1)
-    gather_far(0)
+    relay(0, 1, 0)
+    relay(1, 1, 0)
     close(1)
     release(1)
-    dw(2)
     open_gather(1)
-    relay(1, 0)
+    relay(0, 2, 0)
+    relay(1, 2, 0)
     finish(0, 0)
-    relay(2, 0)
-    dw(2)
-    gather_near(1)
+    gather_near(0, 1)
+    gather_near(1, 1)
+    relay(0, 3, 0)
+    relay(1, 3, 0)
     finish(1, 0)
-    relay(3, 0)
+    gather_far(1)
+    relay(0, 0, 1)
+    relay(1, 0, 1)
     finish(2, 0)
-    relay(0, 1)
+    relay(0, 1, 1)
+    relay(1, 1, 1)
+    relay(0, 2, 1)
+    relay(1, 2, 1)
     finish(3, 0)
-    dw(2)
-    gather_far(1)
-    relay(1, 1)
+    relay(0, 3, 1)
+    relay(1, 3, 1)
     finish(0, 1)
-    dw(STEPS)
-    relay(2, 1)
     finish(1, 1)
-    relay(3, 1)
     finish(2, 1)
     finish(3, 1)
     for w in range(2):
@@ -447,7 +461,7 @@
                 pltpu.VMEM((gr, width), F32),
                 pltpu.VMEM((2, rows, cb), BF16),
                 pltpu.VMEM((2, rows, cb), BF16),
-                dma((3,)),
+                dma((5,)),
                 dma((2, 3)),
                 dma((2, 2)),
                 pltpu.SemaphoreType.REGULAR((2,)),

time: 127 us -> 126 us (level)
  no operation moved by 1% of the time
where the time goes in v3:
time: 126 us
  Pallas kernels  125 us (99%)
    pallas_call x1, Pallas kernels, step(): pl.pallas_call(functools.partial(kernel, side), out_shape=(out(rows, widt...  116 us
    pallas_call x1, Pallas kernels, step(): pl.pallas_call(put_out, out_shape=tuple((jax.ShapeDtypeStruct(h.shape, h....  8.79 us

profile of v3, /device:TPU:97, one launch (start us, length us, event | category | flops | bytes accessed | tf_op | source)
XLA Modules:
  0.0 125.8 jit_solution(8624694390384230212)
XLA Ops:
  0.6 116.2 %shard_map.102 = (bf16[2048,4096]{1,0:T(8,128)(2,1)S(1)}, bf16[4096,384]{1,0:T(8,128)(2,1)S(1)}, bf16[4096,384]{1,0:T(8,128)(2,1)S(1)}, bf16[384,4096]{1,0:T(8,128)(2,1)S(1)}) custom-call(bf16[2048,4096]{1,0:T(8,128)(2,1)} %x_hbm.1, bf16[2048,4096]{1,0:T(8,128)(2,1)} %dy_hbm.1, bf16[2048,384]{1,0:T(8,128)(2,1)} %gate_hbm.1, bf16[2048,384]{1,0:T(8,128)(2,1)} %up_hbm.1, ...), custom_call_target="tpu_custom_call" | custom-call | flops 38654705664 | bytes 83886080 | tf_op jit(solution)/shard_map/pallas_call | solution.py:446
  116.8 8.8 %shard_map.103 = (bf16[2048,4096]{1,0:T(8,128)(2,1)}, bf16[4096,384]{1,0:T(8,128)(2,1)}, bf16[4096,384]{1,0:T(8,128)(2,1)}, bf16[384,4096]{1,0:T(8,128)(2,1)}) custom-call(bf16[2048,4096]{1,0:T(8,128)(2,1)S(1)} %get-tuple-element.8.refs_0_, bf16[4096,384]{1,0:T(8,128)(2,1)S(1)} %get-tuple-element.9.refs_1_, bf16[4096,384]{1,0:T(8,128)(2,1)S(1)} %get-tuple-element.10.refs_2_, ...), custom_call_target="tpu_custom_call" | custom-call | tf_op jit(solution)/shard_map/pallas_call | solution.py:480
